TPU v7x, 256 devices: a whole 4x4x8 slice. The times are simulated.
256 devices in a mesh: gx: 32 (over y, z), gy: 8 (over x, core).
Axes of the slice: x: 4, y: 4, z: 8, core: 2. Of those that a mesh axis runs over, the one named last changes fastest.
Arguments:
- right_side: float32 [64, 128, 4, 3, 128], P('gx', 'gy'), may hold values from -6 to 6
- stencil: float32 [27, 3, 3], replicated, as said below
- class_scale: float32 [8], replicated, may hold values from 0.5 to 4
- material: int32 [64, 128, 128], P('gx', 'gy'), may hold values from 0 to 7
- boundary: int32 [64, 128, 128], P('gx', 'gy'), may hold values 0 or 1
- sign_bits: int32 [64, 128, 3, 128], P('gx', 'gy'), may hold values from 0 to 1
- sample_rows: int32 [32, 8, 128], P('gx', 'gy'), may hold values from 0 to 12287
Outputs:
- solution: float32 [64, 128, 4, 3, 128], P('gx', 'gy')
- residual: float32 [64, 128, 4, 3, 128], P('gx', 'gy')
Inputs may be any that keep to these rules, and one draw needn't show every extreme that they name: In every row of the centre block stencil[13], the diagonal entry exceeds the sum of the magnitudes of all other entries of that row over all 27 blocks.
All inputs are finite; a program needn't handle non-finite values. No bound on the sum of `boundary` on one device may be relied on, other than what follows from the above.
Results may differ from a plain program's by a relative error of at most 0.0028.
Values sent between devices are 32-bit elements; how exact they have to be, the bound alone decides.
No kernel may reach another device: no remote copies, remote signals or barrier semaphores. Data moves between devices by JAX's collectives and lax.ppermute only.
A program may use at most 64 MiB of HBM per device.

v0:
```python
import math
import jax
import jax.numpy as jnp
from jax import lax
from jax.sharding import Mesh
from jax.sharding import PartitionSpec as P

STEPS = 8
GX_GY = ("gx_0", "gx_1", "gy_0", "gy_1")
GX = ("gx_0", "gx_1")
GY = ("gy_0", "gy_1")
exact_mode = lax.Precision.HIGHEST


def padded_2(cells, sides, width):
    for axis, dim in sides:
        count = lax.axis_size(axis)
        ends = count - 1
        head = lax.slice_in_dim(cells, 0, width, axis=dim)
        tail = lax.slice_in_dim(cells, cells.shape[dim] - width, cells.shape[dim], axis=dim)
        cells = jnp.concatenate(
            [
                lax.ppermute(tail, axis, [(i, (i + 1) % count) for i in range(ends)]),
                cells,
                lax.ppermute(head, axis, [((i + 1) % count, i) for i in range(ends)]),
            ],
            axis=dim,
        )
    return cells


def one_axis_at_a_time(shard, axes):
    for axis in axes:
        shard = lax.psum(shard, axis)
    return shard


def hadamard_table():
    lanes = jnp.arange(128, dtype=jnp.int32)
    common = lanes[:, None] & lanes[None, :]
    parity = jnp.zeros((128, 128), jnp.int32)
    for bit in range(7):
        parity = parity + (common >> bit & 1)
    return (1 - 2 * (parity % 2)).astype(jnp.float32) / math.sqrt(128.0)


def material_scale(material, class_scale):
    scale_field = jnp.zeros(material.shape, jnp.float32)
    for number in range(class_scale.shape[0]):
        scale_field = scale_field + jnp.where(
            material == number, class_scale[number], jnp.float32(0.0)
        )
    return scale_field


def extend(field):
    return padded_2(field, ((GX, 0), (GY, 1)), 1)


def operate(field, stencil, scale_field, boundary):
    padded = jnp.pad(extend(field), ((0, 0), (0, 0), (0, 0), (0, 0), (1, 1)))
    extent_x, extent_y, extent_z = (field.shape[0], field.shape[1], field.shape[4])
    summed = jnp.zeros(field.shape, jnp.float32)
    for offset_x in range(3):
        for offset_y in range(3):
            for offset_z in range(3):
                shifted = padded[
                    offset_x : offset_x + extent_x,
                    offset_y : offset_y + extent_y,
                    :,
                    :,
                    offset_z : offset_z + extent_z,
                ]
                coupling = stencil[offset_x * 9 + offset_y * 3 + offset_z]
                summed = summed + jnp.sum(
                    coupling[:, :, None] * shifted[:, :, :, None, :, :], axis=4
                )
    return jnp.where(
        boundary[:, :, None, None, :] == 1, field, scale_field[:, :, None, None, :] * summed
    )


def sketch_local(field, sign_field, picks, table):
    pick_x, pick_y, pick_comp, pick_block, pick_lane = picks
    signed = field * sign_field[:, :, None, :, :]
    tiled = signed.reshape(field.shape[:4] + (field.shape[4] // 128, 128))
    chosen = tiled[pick_x, pick_y, :, pick_comp, pick_block]
    return jnp.sum(chosen * table[pick_lane][:, None, :], axis=-1)


def back_substitute(triangle, projected):
    count = triangle.shape[0]

    def one_row(step, unknowns):
        row = count - 1 - step
        line = triangle[row]
        total = jnp.dot(line[None, :], unknowns, precision=exact_mode)[0]
        value = (projected[row] - total) / line[row]
        return unknowns.at[row].set(value)

    return lax.fori_loop(0, count, one_row, jnp.zeros(projected.shape, jnp.float32))


def solve_small(matrix, rhs):
    count = matrix.shape[1]
    columns = matrix.T

    def one_column(column, state_pair):
        orthonormal, triangle = state_pair
        vector = columns[column]
        first_pass = jnp.dot(orthonormal.T, vector, precision=exact_mode)
        vector = vector - jnp.dot(orthonormal, first_pass, precision=exact_mode)
        second_pass = jnp.dot(orthonormal.T, vector, precision=exact_mode)
        vector = vector - jnp.dot(orthonormal, second_pass, precision=exact_mode)
        length = jnp.sqrt(jnp.sum(vector * vector) + 1e-06)
        orthonormal = orthonormal.at[:, column].set(vector / length)
        triangle = triangle.at[:, column].set((first_pass + second_pass).at[column].set(length))
        return (orthonormal, triangle)

    start = (jnp.zeros(matrix.shape, jnp.float32), jnp.zeros((count, count), jnp.float32))
    orthonormal, triangle = lax.fori_loop(0, count, one_column, start)
    projected = jnp.dot(orthonormal.T, rhs, precision=exact_mode)
    return back_substitute(triangle, projected)


def shards(right_side, stencil, class_scale, material, boundary, sign_bits, sample_rows):
    table = hadamard_table()
    scale_field = material_scale(material, class_scale)
    sign_field = (2 * sign_bits - 1).astype(jnp.float32)
    depth = right_side.shape[4]
    plane = right_side.shape[1] * 3 * depth
    sampled = sample_rows[0, 0]
    rest_y = sampled % plane
    rest_c = rest_y % (3 * depth)
    pick_z = rest_c % depth
    picks = (sampled // plane, rest_y // (3 * depth), rest_c // depth, pick_z // 128, pick_z % 128)
    width = right_side.shape[2]
    local_rhs = sketch_local(right_side, sign_field, picks, table)
    sketch_rhs = one_axis_at_a_time(local_rhs, GX_GY)
    lengths = jnp.sqrt(jnp.sum(sketch_rhs * sketch_rhs, axis=0) + 1e-06)
    basis_block = right_side / lengths[None, None, :, None, None]
    sketch_basis = sketch_rhs / lengths
    blocks = []
    sketched_images = []
    for block_step in range(STEPS):
        operated = operate(basis_block, stencil, scale_field, boundary)
        local_image = sketch_local(operated, sign_field, picks, table)
        sketch_image = one_axis_at_a_time(local_image, GX_GY)
        blocks.append(basis_block)
        sketched_images.append(sketch_image)
        if block_step + 1 < STEPS:
            coupling = jnp.dot(sketch_basis.T, sketch_image, precision=exact_mode)
            remainder = operated - jnp.einsum(
                "xyicz,ij->xyjcz", basis_block, coupling, precision=exact_mode
            )
            sketch_remainder = sketch_image - jnp.dot(sketch_basis, coupling, precision=exact_mode)
            norms = jnp.sqrt(jnp.sum(sketch_remainder * sketch_remainder, axis=0) + 1e-06)
            basis_block = remainder / norms[None, None, :, None, None]
            sketch_basis = sketch_remainder / norms
    matrix = jnp.concatenate(sketched_images, axis=1)
    weights = solve_small(matrix, sketch_rhs)
    solution = jnp.zeros(right_side.shape, jnp.float32)
    for block_step in range(STEPS):
        part_weights = weights[block_step * width : (block_step + 1) * width]
        solution = solution + jnp.einsum(
            "xyicz,ij->xyjcz", blocks[block_step], part_weights, precision=exact_mode
        )
    residual = right_side - operate(solution, stencil, scale_field, boundary)
    return (solution, residual)


def solution(mesh):
    split = Mesh(mesh.devices.reshape(4, 8, 4, 2), ("gx_0", "gx_1", "gy_0", "gy_1"))
    return jax.shard_map(
        shards,
        mesh=split,
        in_specs=(
            P(GX, GY, None, None, None),
            P(),
            P(),
            P(GX, GY, None),
            P(GX, GY, None),
            P(GX, GY, None, None),
            P(GX, GY, None),
        ),
        out_specs=(P(GX, GY, None, None, None), P(GX, GY, None, None, None)),
        check_vma=False,
    )
```

profile of v0, /device:TPU:10, one launch (start us, length us, event | category | flops | bytes accessed | tf_op | source)
XLA Modules:
  0.0 823.2 jit_solution(13014205767853807181)
XLA Ops:
  6.1 8.7 %psum.252 = f32[128,4]{0,1:T(4,128)S(1)} all-reduce(f32[128,4]{0,1:T(4,128)S(1)} %copy.1897), channel_id=1, replica_groups=mesh['gx_0'=4,'gx_1'=8,'gy_0'=4,'gy_1'=2] {'gx_0'}, use_global_device_ids=true, to_apply=%region_1.2 | all-reduce | flops 512 | bytes 4096 | tf_op jit(solution)/shard_map/psum | solution.py:34
  14.8 20.0 %psum.253 = f32[128,4]{0,1:T(4,128)S(1)} all-reduce(f32[128,4]{0,1:T(4,128)S(1)} %psum.252), channel_id=1, replica_groups=mesh['gx_0'=4,'gx_1'=8,'gy_0'=4,'gy_1'=2] {'gx_1'}, use_global_device_ids=true, to_apply=%region_2.3 | all-reduce | flops 512 | bytes 4096 | tf_op jit(solution)/shard_map/psum | solution.py:34
  34.7 8.6 %psum.254 = f32[128,4]{0,1:T(4,128)S(1)} all-reduce(f32[128,4]{0,1:T(4,128)S(1)} %psum.253), channel_id=1, replica_groups=mesh['gx_0'=4,'gx_1'=8,'gy_0'=4,'gy_1'=2] {'gy_0'}, use_global_device_ids=true, to_apply=%region_3.4 | all-reduce | flops 512 | bytes 4096 | tf_op jit(solution)/shard_map/psum | solution.py:34
  72.6 10.2 %psum.256 = f32[128,4]{0,1:T(4,128)S(1)} all-reduce(f32[128,4]{0,1:T(4,128)S(1)} %copy.1900), channel_id=1, replica_groups=mesh['gx_0'=4,'gx_1'=8,'gy_0'=4,'gy_1'=2] {'gx_0'}, use_global_device_ids=true, to_apply=%region_34.35 | all-reduce | flops 512 | bytes 4096 | tf_op jit(solution)/shard_map/psum | solution.py:34
  82.8 16.0 %psum.257 = f32[128,4]{0,1:T(4,128)S(1)} all-reduce(f32[128,4]{0,1:T(4,128)S(1)} %psum.256), channel_id=1, replica_groups=mesh['gx_0'=4,'gx_1'=8,'gy_0'=4,'gy_1'=2] {'gx_1'}, use_global_device_ids=true, to_apply=%region_35.36 | all-reduce | flops 512 | bytes 4096 | tf_op jit(solution)/shard_map/psum | solution.py:34
  98.9 6.7 psum.258
  135.2 7.9 psum.260
  143.1 14.1 %psum.261 = f32[128,4]{0,1:T(4,128)S(1)} all-reduce(f32[128,4]{0,1:T(4,128)S(1)} %psum.260), channel_id=1, replica_groups=mesh['gx_0'=4,'gx_1'=8,'gy_0'=4,'gy_1'=2] {'gx_1'}, use_global_device_ids=true, to_apply=%region_68.69 | all-reduce | flops 512 | bytes 4096 | tf_op jit(solution)/shard_map/psum | solution.py:34
  157.2 7.5 psum.262
  196.0 7.3 psum.264
  203.3 15.0 %psum.265 = f32[128,4]{0,1:T(4,128)S(1)} all-reduce(f32[128,4]{0,1:T(4,128)S(1)} %psum.264), channel_id=1, replica_groups=mesh['gx_0'=4,'gx_1'=8,'gy_0'=4,'gy_1'=2] {'gx_1'}, use_global_device_ids=true, to_apply=%region_101.102 | all-reduce | flops 512 | bytes 4096 | tf_op jit(solution)/shard_map/psum | solution.py:34
  218.3 7.3 psum.266
  263.5 15.6 %psum.269 = f32[128,4]{0,1:T(4,128)S(1)} all-reduce(f32[128,4]{0,1:T(4,128)S(1)} %psum.268), channel_id=1, replica_groups=mesh['gx_0'=4,'gx_1'=8,'gy_0'=4,'gy_1'=2] {'gx_1'}, use_global_device_ids=true, to_apply=%region_134.135 | all-reduce | flops 512 | bytes 4096 | tf_op jit(solution)/shard_map/psum | solution.py:34
  279.1 7.3 psum.270
  324.2 15.8 %psum.273 = f32[128,4]{0,1:T(4,128)S(1)} all-reduce(f32[128,4]{0,1:T(4,128)S(1)} %psum.272), channel_id=1, replica_groups=mesh['gx_0'=4,'gx_1'=8,'gy_0'=4,'gy_1'=2] {'gx_1'}, use_global_device_ids=true, to_apply=%region_167.168 | all-reduce | flops 512 | bytes 4096 | tf_op jit(solution)/shard_map/psum | solution.py:34
  339.9 7.3 psum.274
  385.0 15.8 %psum.277 = f32[128,4]{0,1:T(4,128)S(1)} all-reduce(f32[128,4]{0,1:T(4,128)S(1)} %psum.276), channel_id=1, replica_groups=mesh['gx_0'=4,'gx_1'=8,'gy_0'=4,'gy_1'=2] {'gx_1'}, use_global_device_ids=true, to_apply=%region_200.201 | all-reduce | flops 512 | bytes 4096 | tf_op jit(solution)/shard_map/psum | solution.py:34
  400.7 7.3 psum.278
  445.7 15.8 %psum.281 = f32[128,4]{0,1:T(4,128)S(1)} all-reduce(f32[128,4]{0,1:T(4,128)S(1)} %psum.280), channel_id=1, replica_groups=mesh['gx_0'=4,'gx_1'=8,'gy_0'=4,'gy_1'=2] {'gx_1'}, use_global_device_ids=true, to_apply=%region_233.234 | all-reduce | flops 512 | bytes 4096 | tf_op jit(solution)/shard_map/psum | solution.py:34
  461.5 7.3 psum.282
  506.5 15.8 %psum.285 = f32[128,4]{0,1:T(4,128)S(1)} all-reduce(f32[128,4]{0,1:T(4,128)S(1)} %psum.284), channel_id=1, replica_groups=mesh['gx_0'=4,'gx_1'=8,'gy_0'=4,'gy_1'=2] {'gx_1'}, use_global_device_ids=true, to_apply=%region_266.267 | all-reduce | flops 512 | bytes 4096 | tf_op jit(solution)/shard_map/psum | solution.py:34
  522.3 7.3 psum.286
  532.1 173.4 %while.35 = (s32[]{:T(128)}, f32[128,32]{0,1:T(8,128)S(1)}, f32[32,32]{0,1:T(8,128)S(1)}, f32[32,128]{1,0:T(8,128)S(1)}, s32[]{:T(128)}, /*index=5*/s32[1]{0:T(128)}, f32[]{:T(128)}, s32[]{:T(128)}, s32[1]{0:T(128)}) while((s32[]{:T(128)}, f32[128,32]{0,1:T(8,128)S(1)}, f32[32,32]{0,1:T(8,128)S(1)}, f32[32,128]{1,0:T(8,128)S(1)}, ...), condition=%wide.region_272.273_spmd, body=%wide.region_269.272_spmd.sunk | while | flops 197457 | bytes 72798 | solution.py:121
  705.6 85.4 %while.36 = (s32[]{:T(128)}, f32[32,4]{1,0:T(8,128)S(1)}, f32[32,4]{1,0:T(8,128)S(1)}, f32[32,32]{1,0:T(8,128)S(1)}, s32[]{:T(128)}, /*index=5*/s32[2]{0:T(128)S(1)}, s32[1]{0:T(128)}, s32[]{:T(128)}, s32[]{:T(128)}, s32[]{:T(128)}) while((s32[]{:T(128)}, f32[32,4]{1,0:T(8,128)S(1)}, f32[32,4]{1,0:T(8,128)S(1)}, ...), condition=%wide.region_275.276_spmd, body=%wide.region_273.275_spmd.sunk | while | flops 1564 | bytes 20220 | solution.py:101
  (993 shorter events, 531.2 us)
Async XLA Ops:
  46.0 12.2 %collective-permute-start.1 = (f32[1,16,4,3,128]{4,1,3,2,0:T(8,128)S(1)}, f32[1,16,4,3,128]{4,1,3,2,0:T(8,128)S(1)}, u32[]{:S(2)}, u32[]{:S(2)}) collective-permute-start(f32[1,16,4,3,128]{4,1,3,2,0:T(8,128)S(1)} %get-tuple-element.683), channel_id=1, source_target_pairs={{8,0},{16,8},{24,16},{32,24},{40,32},{48,40},{56,48},{64,56},{72,6... | collective-permute-start | bytes 294920 | tf_op jit(solution)/shard_map/ppermute | solution.py:25
  49.7 8.6 %collective-permute-start = (f32[1,16,4,3,128]{4,1,3,2,0:T(8,128)S(1)}, f32[1,16,4,3,128]{4,1,3,2,0:T(8,128)S(1)}, u32[]{:S(2)}, u32[]{:S(2)}) collective-permute-start(f32[1,16,4,3,128]{4,1,3,2,0:T(8,128)S(1)} %get-tuple-element.682), channel_id=1, source_target_pairs={{0,8},{8,16},{16,24},{24,32},{32,40},{40,48},{48,56},{56,64},{64,7... | collective-permute-start | bytes 294920 | tf_op jit(solution)/shard_map/ppermute | solution.py:23
  58.4 5.5 collective-permute-start.3
  109.3 6.8 collective-permute-start.5
  111.2 8.9 %collective-permute-start.4 = (f32[1,16,4,3,128]{4,1,3,2,0:T(8,128)S(1)}, f32[1,16,4,3,128]{4,1,3,2,0:T(8,128)S(1)}, u32[]{:S(2)}, u32[]{:S(2)}) collective-permute-start(f32[1,16,4,3,128]{4,1,3,2,0:T(8,128)S(1)} %get-tuple-element.678), channel_id=1, source_target_pairs={{0,8},{8,16},{16,24},{24,32},{32,40},{40,48},{48,56},{56,64},{64,7... | collective-permute-start | bytes 294920 | tf_op jit(solution)/shard_map/ppermute | solution.py:23
  120.1 6.2 collective-permute-start.7
  168.4 7.0 collective-permute-start.9
  173.1 8.6 %collective-permute-start.8 = (f32[1,16,4,3,128]{4,1,3,2,0:T(8,128)S(1)}, f32[1,16,4,3,128]{4,1,3,2,0:T(8,128)S(1)}, u32[]{:S(2)}, u32[]{:S(2)}) collective-permute-start(f32[1,16,4,3,128]{4,1,3,2,0:T(8,128)S(1)} %get-tuple-element.674), channel_id=1, source_target_pairs={{0,8},{8,16},{16,24},{24,32},{32,40},{40,48},{48,56},{56,64},{64,7... | collective-permute-start | bytes 294920 | tf_op jit(solution)/shard_map/ppermute | solution.py:23
  181.8 5.2 collective-permute-start.11
  229.3 7.6 collective-permute-start.13
  234.5 8.6 %collective-permute-start.12 = (f32[1,16,4,3,128]{4,1,3,2,0:T(8,128)S(1)}, f32[1,16,4,3,128]{4,1,3,2,0:T(8,128)S(1)}, u32[]{:S(2)}, u32[]{:S(2)}) collective-permute-start(f32[1,16,4,3,128]{4,1,3,2,0:T(8,128)S(1)} %get-tuple-element.670), channel_id=1, source_target_pairs={{0,8},{8,16},{16,24},{24,32},{32,40},{40,48},{48,56},{56,64},{64,7... | collective-permute-start | bytes 294920 | tf_op jit(solution)/shard_map/ppermute | solution.py:23
  245.6 5.2 collective-permute-start.14
  290.1 7.6 collective-permute-start.17
  295.3 8.6 %collective-permute-start.16 = (f32[1,16,4,3,128]{4,1,3,2,0:T(8,128)S(1)}, f32[1,16,4,3,128]{4,1,3,2,0:T(8,128)S(1)}, u32[]{:S(2)}, u32[]{:S(2)}) collective-permute-start(f32[1,16,4,3,128]{4,1,3,2,0:T(8,128)S(1)} %get-tuple-element.666), channel_id=1, source_target_pairs={{0,8},{8,16},{16,24},{24,32},{32,40},{40,48},{48,56},{56,64},{64,7... | collective-permute-start | bytes 294920 | tf_op jit(solution)/shard_map/ppermute | solution.py:23
  350.9 7.6 collective-permute-start.21
  356.1 8.6 %collective-permute-start.20 = (f32[1,16,4,3,128]{4,1,3,2,0:T(8,128)S(1)}, f32[1,16,4,3,128]{4,1,3,2,0:T(8,128)S(1)}, u32[]{:S(2)}, u32[]{:S(2)}) collective-permute-start(f32[1,16,4,3,128]{4,1,3,2,0:T(8,128)S(1)} %get-tuple-element.662), channel_id=1, source_target_pairs={{0,8},{8,16},{16,24},{24,32},{32,40},{40,48},{48,56},{56,64},{64,7... | collective-permute-start | bytes 294920 | tf_op jit(solution)/shard_map/ppermute | solution.py:23
  411.7 7.6 collective-permute-start.25
  416.9 8.6 %collective-permute-start.24 = (f32[1,16,4,3,128]{4,1,3,2,0:T(8,128)S(1)}, f32[1,16,4,3,128]{4,1,3,2,0:T(8,128)S(1)}, u32[]{:S(2)}, u32[]{:S(2)}) collective-permute-start(f32[1,16,4,3,128]{4,1,3,2,0:T(8,128)S(1)} %get-tuple-element.658), channel_id=1, source_target_pairs={{0,8},{8,16},{16,24},{24,32},{32,40},{40,48},{48,56},{56,64},{64,7... | collective-permute-start | bytes 294920 | tf_op jit(solution)/shard_map/ppermute | solution.py:23
  472.5 7.6 collective-permute-start.29
  477.7 8.6 %collective-permute-start.28 = (f32[1,16,4,3,128]{4,1,3,2,0:T(8,128)S(1)}, f32[1,16,4,3,128]{4,1,3,2,0:T(8,128)S(1)}, u32[]{:S(2)}, u32[]{:S(2)}) collective-permute-start(f32[1,16,4,3,128]{4,1,3,2,0:T(8,128)S(1)} %get-tuple-element.654), channel_id=1, source_target_pairs={{0,8},{8,16},{16,24},{24,32},{32,40},{40,48},{48,56},{56,64},{64,7... | collective-permute-start | bytes 294920 | tf_op jit(solution)/shard_map/ppermute | solution.py:23
  488.8 5.2 collective-permute-start.30
  796.2 7.6 collective-permute-start.33
  801.4 8.6 %collective-permute-start.32 = (f32[1,16,4,3,128]{4,1,3,2,0:T(8,128)S(1)}, f32[1,16,4,3,128]{4,1,3,2,0:T(8,128)S(1)}, u32[]{:S(2)}, u32[]{:S(2)}) collective-permute-start(f32[1,16,4,3,128]{4,1,3,2,0:T(8,128)S(1)} %get-tuple-element.650), channel_id=1, source_target_pairs={{0,8},{8,16},{16,24},{24,32},{32,40},{40,48},{48,56},{56,64},{64,7... | collective-permute-start | bytes 294920 | tf_op jit(solution)/shard_map/ppermute | solution.py:23
  812.5 5.2 collective-permute-start.34
  (18 other events, 502.4 us)
where the time goes:
time: 833 us; the launch traced here: 823 us
  blocking collectives  299 us (36%)
  other arithmetic  135 us (16%)
  starting transfers between devices  105 us (13%)
  matrix products  93 us (11%)
  waiting for transfers between devices  76.8 us (9%)
  local copies, waits for them, and re-layouts  67.1 us (8%)
  loops' own time  44.2 us (5%)
    psum x36, blocking collectives, one_axis_at_a_time(): shard = lax.psum(shard, axis)  299 us
    another operation x128, other arithmetic  87.4 us
    ppermute x18, waiting for transfers between devices, padded_2(): lax.ppermute(tail, axis, [(i, (i + 1) % count) for i in range(ends)])  73.7 us
    ppermute x18, starting transfers between devices, padded_2(): lax.ppermute(head, axis, [((i + 1) % count, i) for i in range(ends)])  66.7 us
    another operation x1, loops' own time, solve_small(): orthonormal, triangle = lax.fori_loop(0, count, one_column, start)  43.5 us
    dot_general x32, matrix products, one_row(): total = jnp.dot(line[None, :], unknowns, precision=exact_mode)[0]  42.8 us
    ppermute x18, starting transfers between devices, padded_2(): lax.ppermute(tail, axis, [(i, (i + 1) % count) for i in range(ends)])  38 us
    dot_general x32, matrix products, one_column(): vector = vector - jnp.dot(orthonormal, second_pass, precision=exact_mode)  25.2 us
  transfers between devices with their start and end apart: 36, of which 25 were waited for; matrix products, arithmetic and copies ran while one was open for 1% of the time, Pallas kernels for 0%

commit v1 on v0

--- a/solution.py
+++ b/solution.py
@@ -31,7 +31,11 @@
 
 def one_axis_at_a_time(shard, axes):
     for axis in axes:
-        shard = lax.psum(shard, axis)
+
+        def goods_close(x_local, mesh_ax):
+            return jnp.sum(lax.all_gather(x_local, mesh_ax), axis=0)
+
+        shard = goods_close(shard, axis)
     return shard
 
 

time: 833 us -> 923 us (1.11)
  blocking collectives: 299 us -> 408 us
  starting transfers between devices: 105 us -> 94.2 us
    all_gather x0 -> x36, blocking collectives: none -> 408 us  [goods_close(): return jnp.sum(lax.all_gather(x_local, mesh_ax), axis=0)]
    psum x36 -> x0, blocking collectives: 299 us -> none  [one_axis_at_a_time(): shard = lax.psum(shard, axis)]
    ppermute x18, starting transfers between devices: 66.7 us -> 48 us  [padded_2(): lax.ppermute(head, axis, [((i + 1) % count, i) for i in range(ends)])]
    ppermute x18, waiting for transfers between devices: 73.7 us -> 62.5 us  [padded_2(): lax.ppermute(tail, axis, [(i, (i + 1) % count) for i in range(ends)])]
where the time goes in v1:
time: 923 us; the launch traced here: 914 us
  blocking collectives  408 us (44%)
  other arithmetic  135 us (15%)
  starting transfers between devices  94.2 us (10%)
  matrix products  93 us (10%)
  waiting for transfers between devices  68.4 us (7%)
  local copies, waits for them, and re-layouts  67.5 us (7%)
  loops' own time  44.2 us (5%)
    all_gather x36, blocking collectives, goods_close(): return jnp.sum(lax.all_gather(x_local, mesh_ax), axis=0)  408 us
    another operation x128, other arithmetic  87.4 us
    ppermute x18, waiting for transfers between devices, padded_2(): lax.ppermute(tail, axis, [(i, (i + 1) % count) for i in range(ends)])  62.5 us
    ppermute x18, starting transfers between devices, padded_2(): lax.ppermute(head, axis, [((i + 1) % count, i) for i in range(ends)])  48 us
    ppermute x18, starting transfers between devices, padded_2(): lax.ppermute(tail, axis, [(i, (i + 1) % count) for i in range(ends)])  46.2 us
    another operation x1, loops' own time, solve_small(): orthonormal, triangle = lax.fori_loop(0, count, one_column, start)  43.5 us
    dot_general x32, matrix products, one_row(): total = jnp.dot(line[None, :], unknowns, precision=exact_mode)[0]  42.8 us
    dot_general x32, matrix products, one_column(): vector = vector - jnp.dot(orthonormal, second_pass, precision=exact_mode)  25.2 us
  transfers between devices with their start and end apart: 36, of which 25 were waited for; matrix products, arithmetic and copies ran while one was open for 1% of the time, Pallas kernels for 0%

profile of v1, /device:TPU:10, one launch (start us, length us, event | category | flops | bytes accessed | tf_op | source)
XLA Modules:
  0.0 913.7 jit_solution(8915826757414846021)
XLA Ops:
  6.0 12.5 %all-gather = f32[512,4]{1,0:T(8,128)S(1)} all-gather(f32[128,4]{1,0:T(8,128)S(1)} %multiply_reduce_fusion.252), channel_id=2, replica_groups=mesh['gx_0'=4,'gx_1'=8,'gy_0'=4,'gy_1'=2] {'gx_0'}, dimensions={0}, use_global_device_ids=true | all-gather | bytes 10240 | tf_op jit(solution)/shard_map/all_gather | solution.py:36
  18.6 25.6 %all-gather.1 = f32[1024,4]{0,1:T(4,128)S(1)} all-gather(f32[128,4]{0,1:T(4,128)S(1)} %bitcast_reduce_fusion.26), channel_id=3, replica_groups=mesh['gx_0'=4,'gx_1'=8,'gy_0'=4,'gy_1'=2] {'gx_1'}, dimensions={0}, use_global_device_ids=true | all-gather | bytes 18432 | tf_op jit(solution)/shard_map/all_gather | solution.py:36
  44.2 10.9 %all-gather.2 = f32[512,4]{0,1:T(4,128)S(1)} all-gather(f32[128,4]{0,1:T(4,128)S(1)} %bitcast_reduce_fusion.8), channel_id=4, replica_groups=mesh['gx_0'=4,'gx_1'=8,'gy_0'=4,'gy_1'=2] {'gy_0'}, dimensions={0}, use_global_device_ids=true | all-gather | bytes 10240 | tf_op jit(solution)/shard_map/all_gather | solution.py:36
  82.1 12.3 %all-gather.4 = f32[512,4]{1,0:T(8,128)S(1)} all-gather(f32[128,4]{1,0:T(8,128)S(1)} %multiply_reduce_fusion.251), channel_id=6, replica_groups=mesh['gx_0'=4,'gx_1'=8,'gy_0'=4,'gy_1'=2] {'gx_0'}, dimensions={0}, use_global_device_ids=true | all-gather | bytes 10240 | tf_op jit(solution)/shard_map/all_gather | solution.py:36
  94.5 21.3 %all-gather.5 = f32[1024,4]{0,1:T(4,128)S(1)} all-gather(f32[128,4]{0,1:T(4,128)S(1)} %bitcast_reduce_fusion.24), channel_id=7, replica_groups=mesh['gx_0'=4,'gx_1'=8,'gy_0'=4,'gy_1'=2] {'gx_1'}, dimensions={0}, use_global_device_ids=true | all-gather | bytes 18432 | tf_op jit(solution)/shard_map/all_gather | solution.py:36
  115.8 10.2 %all-gather.6 = f32[512,4]{0,1:T(4,128)S(1)} all-gather(f32[128,4]{0,1:T(4,128)S(1)} %bitcast_reduce_fusion.7), channel_id=8, replica_groups=mesh['gx_0'=4,'gx_1'=8,'gy_0'=4,'gy_1'=2] {'gy_0'}, dimensions={0}, use_global_device_ids=true | all-gather | bytes 10240 | tf_op jit(solution)/shard_map/all_gather | solution.py:36
  156.3 11.0 %all-gather.8 = f32[512,4]{1,0:T(8,128)S(1)} all-gather(f32[128,4]{1,0:T(8,128)S(1)} %multiply_reduce_fusion.250), channel_id=10, replica_groups=mesh['gx_0'=4,'gx_1'=8,'gy_0'=4,'gy_1'=2] {'gx_0'}, dimensions={0}, use_global_device_ids=true | all-gather | bytes 10240 | tf_op jit(solution)/shard_map/all_gather | solution.py:36
  167.4 21.0 %all-gather.9 = f32[1024,4]{0,1:T(4,128)S(1)} all-gather(f32[128,4]{0,1:T(4,128)S(1)} %bitcast_reduce_fusion.22), channel_id=11, replica_groups=mesh['gx_0'=4,'gx_1'=8,'gy_0'=4,'gy_1'=2] {'gx_1'}, dimensions={0}, use_global_device_ids=true | all-gather | bytes 18432 | tf_op jit(solution)/shard_map/all_gather | solution.py:36
  226.2 11.7 %all-gather.12 = f32[512,4]{1,0:T(8,128)S(1)} all-gather(f32[128,4]{1,0:T(8,128)S(1)} %multiply_reduce_fusion.249), channel_id=14, replica_groups=mesh['gx_0'=4,'gx_1'=8,'gy_0'=4,'gy_1'=2] {'gx_0'}, dimensions={0}, use_global_device_ids=true | all-gather | bytes 10240 | tf_op jit(solution)/shard_map/all_gather | solution.py:36
  238.0 21.0 %all-gather.13 = f32[1024,4]{0,1:T(4,128)S(1)} all-gather(f32[128,4]{0,1:T(4,128)S(1)} %bitcast_reduce_fusion.20), channel_id=15, replica_groups=mesh['gx_0'=4,'gx_1'=8,'gy_0'=4,'gy_1'=2] {'gx_1'}, dimensions={0}, use_global_device_ids=true | all-gather | bytes 18432 | tf_op jit(solution)/shard_map/all_gather | solution.py:36
  297.1 11.6 %all-gather.16 = f32[512,4]{1,0:T(8,128)S(1)} all-gather(f32[128,4]{1,0:T(8,128)S(1)} %multiply_reduce_fusion.248), channel_id=18, replica_groups=mesh['gx_0'=4,'gx_1'=8,'gy_0'=4,'gy_1'=2] {'gx_0'}, dimensions={0}, use_global_device_ids=true | all-gather | bytes 10240 | tf_op jit(solution)/shard_map/all_gather | solution.py:36
  308.9 21.0 %all-gather.17 = f32[1024,4]{0,1:T(4,128)S(1)} all-gather(f32[128,4]{0,1:T(4,128)S(1)} %bitcast_reduce_fusion.18), channel_id=19, replica_groups=mesh['gx_0'=4,'gx_1'=8,'gy_0'=4,'gy_1'=2] {'gx_1'}, dimensions={0}, use_global_device_ids=true | all-gather | bytes 18432 | tf_op jit(solution)/shard_map/all_gather | solution.py:36
  329.9 10.2 %all-gather.18 = f32[512,4]{0,1:T(4,128)S(1)} all-gather(f32[128,4]{0,1:T(4,128)S(1)} %bitcast_reduce_fusion.4), channel_id=20, replica_groups=mesh['gx_0'=4,'gx_1'=8,'gy_0'=4,'gy_1'=2] {'gy_0'}, dimensions={0}, use_global_device_ids=true | all-gather | bytes 10240 | tf_op jit(solution)/shard_map/all_gather | solution.py:36
  367.8 11.8 %all-gather.20 = f32[512,4]{1,0:T(8,128)S(1)} all-gather(f32[128,4]{1,0:T(8,128)S(1)} %multiply_reduce_fusion.247), channel_id=22, replica_groups=mesh['gx_0'=4,'gx_1'=8,'gy_0'=4,'gy_1'=2] {'gx_0'}, dimensions={0}, use_global_device_ids=true | all-gather | bytes 10240 | tf_op jit(solution)/shard_map/all_gather | solution.py:36
  379.7 21.0 %all-gather.21 = f32[1024,4]{0,1:T(4,128)S(1)} all-gather(f32[128,4]{0,1:T(4,128)S(1)} %bitcast_reduce_fusion.16), channel_id=23, replica_groups=mesh['gx_0'=4,'gx_1'=8,'gy_0'=4,'gy_1'=2] {'gx_1'}, dimensions={0}, use_global_device_ids=true | all-gather | bytes 18432 | tf_op jit(solution)/shard_map/all_gather | solution.py:36
  439.1 11.3 %all-gather.24 = f32[512,4]{1,0:T(8,128)S(1)} all-gather(f32[128,4]{1,0:T(8,128)S(1)} %multiply_reduce_fusion.246), channel_id=26, replica_groups=mesh['gx_0'=4,'gx_1'=8,'gy_0'=4,'gy_1'=2] {'gx_0'}, dimensions={0}, use_global_device_ids=true | all-gather | bytes 10240 | tf_op jit(solution)/shard_map/all_gather | solution.py:36
  450.5 21.0 %all-gather.25 = f32[1024,4]{0,1:T(4,128)S(1)} all-gather(f32[128,4]{0,1:T(4,128)S(1)} %bitcast_reduce_fusion.14), channel_id=27, replica_groups=mesh['gx_0'=4,'gx_1'=8,'gy_0'=4,'gy_1'=2] {'gx_1'}, dimensions={0}, use_global_device_ids=true | all-gather | bytes 18432 | tf_op jit(solution)/shard_map/all_gather | solution.py:36
  471.6 10.2 %all-gather.26 = f32[512,4]{0,1:T(4,128)S(1)} all-gather(f32[128,4]{0,1:T(4,128)S(1)} %bitcast_reduce_fusion.2), channel_id=28, replica_groups=mesh['gx_0'=4,'gx_1'=8,'gy_0'=4,'gy_1'=2] {'gy_0'}, dimensions={0}, use_global_device_ids=true | all-gather | bytes 10240 | tf_op jit(solution)/shard_map/all_gather | solution.py:36
  509.9 11.4 %all-gather.28 = f32[512,4]{1,0:T(8,128)S(1)} all-gather(f32[128,4]{1,0:T(8,128)S(1)} %multiply_reduce_fusion.245), channel_id=30, replica_groups=mesh['gx_0'=4,'gx_1'=8,'gy_0'=4,'gy_1'=2] {'gx_0'}, dimensions={0}, use_global_device_ids=true | all-gather | bytes 10240 | tf_op jit(solution)/shard_map/all_gather | solution.py:36
  521.4 21.0 %all-gather.29 = f32[1024,4]{0,1:T(4,128)S(1)} all-gather(f32[128,4]{0,1:T(4,128)S(1)} %bitcast_reduce_fusion.12), channel_id=31, replica_groups=mesh['gx_0'=4,'gx_1'=8,'gy_0'=4,'gy_1'=2] {'gx_1'}, dimensions={0}, use_global_device_ids=true | all-gather | bytes 18432 | tf_op jit(solution)/shard_map/all_gather | solution.py:36
  580.6 11.2 %all-gather.32 = f32[512,4]{1,0:T(8,128)S(1)} all-gather(f32[128,4]{1,0:T(8,128)S(1)} %multiply_reduce_fusion.244), channel_id=34, replica_groups=mesh['gx_0'=4,'gx_1'=8,'gy_0'=4,'gy_1'=2] {'gx_0'}, dimensions={0}, use_global_device_ids=true | all-gather | bytes 10240 | tf_op jit(solution)/shard_map/all_gather | solution.py:36
  591.9 21.0 %all-gather.33 = f32[1024,4]{0,1:T(4,128)S(1)} all-gather(f32[128,4]{0,1:T(4,128)S(1)} %bitcast_reduce_fusion.10), channel_id=35, replica_groups=mesh['gx_0'=4,'gx_1'=8,'gy_0'=4,'gy_1'=2] {'gx_1'}, dimensions={0}, use_global_device_ids=true | all-gather | bytes 18432 | tf_op jit(solution)/shard_map/all_gather | solution.py:36
  625.1 173.4 %while.35 = (s32[]{:T(128)}, f32[128,32]{0,1:T(8,128)S(1)}, f32[32,32]{0,1:T(8,128)S(1)}, f32[32,128]{1,0:T(8,128)S(1)}, s32[]{:T(128)}, /*index=5*/s32[1]{0:T(128)}, f32[]{:T(128)}, s32[]{:T(128)}, s32[1]{0:T(128)}) while((s32[]{:T(128)}, f32[128,32]{0,1:T(8,128)S(1)}, f32[32,32]{0,1:T(8,128)S(1)}, f32[32,128]{1,0:T(8,128)S(1)}, ...), condition=%wide.region_272.273_spmd, body=%wide.region_269.272_spmd.sunk | while | flops 197457 | bytes 72798 | solution.py:125
  798.7 85.4 %while.36 = (s32[]{:T(128)}, f32[32,4]{1,0:T(8,128)S(1)}, f32[32,4]{1,0:T(8,128)S(1)}, f32[32,32]{1,0:T(8,128)S(1)}, s32[]{:T(128)}, /*index=5*/s32[2]{0:T(128)S(1)}, s32[1]{0:T(128)}, s32[]{:T(128)}, s32[]{:T(128)}, s32[]{:T(128)}) while((s32[]{:T(128)}, f32[32,4]{1,0:T(8,128)S(1)}, f32[32,4]{1,0:T(8,128)S(1)}, ...), condition=%wide.region_275.276_spmd, body=%wide.region_273.275_spmd.sunk | while | flops 1564 | bytes 20220 | solution.py:105
  (1029 shorter events, 525.7 us)
Async XLA Ops:
  57.2 12.2 %collective-permute-start.1 = (f32[1,16,4,3,128]{4,1,3,2,0:T(8,128)S(1)}, f32[1,16,4,3,128]{4,1,3,2,0:T(8,128)S(1)}, u32[]{:S(2)}, u32[]{:S(2)}) collective-permute-start(f32[1,16,4,3,128]{4,1,3,2,0:T(8,128)S(1)} %get-tuple-element.683), channel_id=1, source_target_pairs={{8,0},{16,8},{24,16},{32,24},{40,32},{48,40},{56,48},{64,56},{72,6... | collective-permute-start | bytes 294920 | tf_op jit(solution)/shard_map/ppermute | solution.py:25
  60.5 8.9 collective-permute-start
  129.1 7.8 collective-permute-start.5
  134.5 8.6 collective-permute-start.4
  201.8 6.8 collective-permute-start.9
  204.5 8.6 collective-permute-start.8
  215.1 5.1 collective-permute-start.10
  272.4 6.8 collective-permute-start.13
  275.4 8.6 collective-permute-start.12
  286.0 5.1 collective-permute-start.14
  343.2 6.8 collective-permute-start.17
  346.1 8.6 collective-permute-start.16
  356.7 5.1 collective-permute-start.18
  414.0 6.8 collective-permute-start.21
  417.5 8.6 collective-permute-start.20
  484.9 6.8 collective-permute-start.25
  488.2 8.6 collective-permute-start.24
  498.8 5.1 collective-permute-start.26
  555.7 6.8 collective-permute-start.29
  559.0 8.6 collective-permute-start.28
  569.6 5.1 collective-permute-start.30
  889.2 6.8 collective-permute-start.33
  892.4 8.6 collective-permute-start.32
  903.0 5.1 collective-permute-start.34
  (18 other events, 564.1 us)
